TPU v7x, 32 devices: a whole 2x2x4 slice. The times are simulated.
32 devices in a mesh: groups: 2 (over y), row: 4 (over z), col: 2 (over x), sub: 2 (over core).
Axes of the slice: x: 2, y: 2, z: 4, core: 2. Of those that a mesh axis runs over, the one named last changes fastest.
Arguments:
- matrix: float32 [16384, 8192], P(('groups', 'row'), ('col', 'sub')), parts along dimension 0, may hold values from -60 to 60
- basis_vectors: float32 [16384, 1024], P(('groups', 'row'), ('col', 'sub')), parts along dimension 0, may hold values from -0.0625 to 0.0625
- split_size: int32 [2], P('groups'), parts along dimension 0, may hold values from 256 to 767
Outputs:
- children: float32 [2, 2048, 1024], P('sub', ('groups', 'row'), 'col'), parts along dimension 1
There are 2 independent parts, one for each index of `groups`. A program takes and returns all parts, laid end to end along the dimension named above; each array names one. Nothing has to cross between parts.
Inputs may be any that keep to these rules, and one draw needn't show every extreme that they name: The second subspace has 1024 minus split_size vectors.
All inputs are finite; a program needn't handle non-finite values.
Results may differ from a plain program's by a relative error of at most 0.00011.
Values sent between devices are 32-bit elements; how exact they have to be, the bound alone decides.
A program may use at most 128 MiB of HBM per device.

v0:
```python
import jax
import jax.numpy as jnp
from jax import lax
from jax.sharding import PartitionSpec as P


def shards(matrix, basis_vectors, split_size):
    strip = lax.all_gather(basis_vectors, "row", axis=0, tiled=True)
    row_panel = lax.all_to_all(strip, ("col", "sub"), split_axis=0, concat_axis=1, tiled=True)
    partial_image = jnp.dot(
        matrix, row_panel, precision=lax.Precision.HIGHEST, preferred_element_type=jnp.float32
    )
    image = lax.psum_scatter(partial_image, ("col", "sub"), scatter_dimension=1, tiled=True)
    partial_proj = lax.dot_general(
        lax.all_gather(basis_vectors, ("col", "sub"), axis=1, tiled=True),
        image,
        (((0,), (0,)), ((), ())),
        precision=lax.Precision.HIGHEST,
        preferred_element_type=jnp.float32,
    )
    proj_block = lax.psum_scatter(partial_proj, "row", scatter_dimension=0, tiled=True)
    child_block = lax.all_gather(proj_block, "sub", axis=1, tiled=True)
    row_ids = (
        jnp.arange(child_block.shape[0], dtype=jnp.int32)
        + lax.axis_index("row") * child_block.shape[0]
    )
    col_ids = (
        jnp.arange(child_block.shape[1], dtype=jnp.int32)
        + lax.axis_index("col") * child_block.shape[1]
    )
    leading = split_size[0]
    row_first = row_ids < leading
    col_first = col_ids < leading
    mask_one = row_first[:, None] & col_first[None, :]
    mask_two = jnp.logical_not(row_first)[:, None] & jnp.logical_not(col_first)[None, :]
    selected = jnp.where(lax.axis_index("sub") == 0, mask_one, mask_two)
    return jnp.where(selected, child_block, jnp.zeros((), jnp.float32))[None]


def solution(mesh):
    placed = (
        P(("groups", "row"), ("col", "sub")),
        P(("groups", "row"), ("col", "sub")),
        P("groups"),
    )
    return jax.shard_map(
        shards,
        mesh=mesh,
        in_specs=placed,
        out_specs=P("sub", ("groups", "row"), "col"),
        check_vma=False,
    )
```

profile of v0, /device:TPU:0, one launch (start us, length us, event | category | flops | bytes accessed | tf_op | source)
XLA Modules:
  0.0 493.2 jit_solution(18207130917740719552)
XLA Ops:
  6.5 0.0 all-gather.3.cloned.1.call-start
  6.5 0.7 all-gather.3.cloned.1.call-update
  7.3 0.0 all-gather.5.cloned.1.call-start
  7.3 0.7 all-gather.5.cloned.1.call-update
  8.0 0.0 reduce-scatter.3.cloned.1.call-start
  8.1 153.2 %all-gather.3.cloned.1.call-done = f32[8192,256]{1,0:T(8,128)} async-done(((f32[2048,256]{1,0:T(8,128)}), f32[8192,256]{1,0:T(8,128)}) %all-gather.3.cloned.1.call-update) | async-done | bytes 8388624 | tf_op jit(solution)/shard_map/all_gather | solution.py:8
  161.3 145.5 %all_to_all.19 = f32[4,2048,256]{2,1,0:T(8,128)} all-to-all(f32[4,2048,256]{2,1,0:T(8,128)} %bitcast.15), channel_id=1, replica_groups=mesh['groups'=2,'row'=4,'col'=2,'sub'=2] {'col','sub'}, dimensions={0} | all-to-all | bytes 16777216 | tf_op jit(solution)/shard_map/all_to_all | solution.py:9
  306.7 8.8 %copy.6 = f32[2048,4,256]{0,2,1:T(8,128)} copy(f32[2048,4,256]{2,0,1:T(8,128)} %bitcast.14) | data formatting | bytes 16777216 | tf_op jit(solution)/shard_map/all_to_all | solution.py:9
  315.5 60.4 %fusion.2 = f32[2048,1024]{1,0:T(8,128)} fusion(f32[2048,2048]{1,0:T(8,128)} %param.3, f32[2048,1024]{0,1:T(8,128)} %bitcast.16), kind=kOutput, calls=%fused_computation.6 | convolution fusion | flops 51539607552 | bytes 33554432 | tf_op jit(solution)/shard_map/dot_general | solution.py:10
  376.0 0.0 reduce-scatter.3.cloned.1.call-update
  376.0 0.2 reduce-scatter.5.cloned.1.call-start
  376.2 0.0 all-gather.5.cloned.1.call-done
  376.2 68.4 %reduce-scatter.3.cloned.1.call-done = f32[2048,256]{1,0:T(8,128)} async-done(((f32[2048,1024]{1,0:T(8,128)}), f32[2048,256]{1,0:T(8,128)}) %reduce-scatter.3.cloned.1.call-update) | async-done | bytes 2097168 | tf_op jit(solution)/shard_map/reduce_scatter | solution.py:13
  444.6 11.0 %convolution_bitcast_fusion = f32[1024,256]{0,1:T(8,128)} fusion(f32[2048,256]{1,0:T(8,128)} %reduce-scatter.3.cloned.1.call-done, f32[2048,1024]{1,0:T(8,128)} %all-gather.5.cloned.1.call-done), kind=kOutput, calls=%fused_computation | convolution fusion | flops 6442450944 | bytes 11534336 | tf_op jit(solution)/shard_map/dot_general | solution.py:14
  455.6 0.0 reduce-scatter.5.cloned.1.call-update
  456.3 26.8 %reduce-scatter.5.cloned.1.call-done = f32[256,256]{0,1:T(8,128)} async-done(((f32[1024,256]{0,1:T(8,128)}), f32[256,256]{0,1:T(8,128)}) %reduce-scatter.5.cloned.1.call-update) | async-done | bytes 262160 | tf_op jit(solution)/shard_map/reduce_scatter | solution.py:21
  483.1 2.4 all_gather.11
  485.5 0.2 select_bitcast_fusion
  485.7 1.0 copy.7
  (2 shorter events, 0.0 us)
Async XLA Ops:
  6.5 154.7 %all-gather.3.cloned.1.call-start = ((), (), s32[]{:S(2)}) async-start(), calls=%async_computation.3 | async-start | bytes 10485760 | tf_op jit(solution)/shard_map/all_gather | solution.py:8
  7.3 369.0 %all-gather.5.cloned.1.call-start = ((), (), s32[]{:S(2)}) async-start(), calls=%async_computation.5 | async-start | bytes 10485760 | tf_op jit(solution)/shard_map/all_gather | solution.py:15
  8.0 436.6 %reduce-scatter.3.cloned.1.call-start = ((), (), s32[]{:S(2)}) async-start(), calls=%async_computation.4 | async-start | bytes 10485760 | tf_op jit(solution)/shard_map/reduce_scatter | solution.py:13
  376.0 107.1 %reduce-scatter.5.cloned.1.call-start = ((), (), s32[]{:S(2)}) async-start(), calls=%async_computation.6 | async-start | bytes 1310720 | tf_op jit(solution)/shard_map/reduce_scatter | solution.py:21
Sparse Core Ops, SparseCore 0:
  8.9 152.3 all-gather.2
  162.8 101.4 all-gather.4
  376.1 68.5 reduce-scatter.2
  455.8 27.2 reduce-scatter.4
where the time goes:
time: 494 us; the launch traced here: 493 us
  waiting for transfers between devices  250 us (51%)
  blocking collectives  148 us (30%)
  matrix products  71.4 us (14%)
  between operations  13.8 us (3%)
  local copies, waits for them, and re-layouts  9.76 us (2%)
    all_gather x1, waiting for transfers between devices, shards(): strip = lax.all_gather(basis_vectors, 'row', axis=0, tiled=True)  153 us
    all_to_all x1, blocking collectives, shards(): lax.all_to_all(strip, ('col', 'sub'), split_axis=0, concat_axis=1, tiled=...  145 us
    reduce_scatter x1, waiting for transfers between devices, shards(): lax.psum_scatter(partial_image, ('col', 'sub'), scatter_dimension=1, tile...  68.4 us
    dot_general x1, matrix products, shards(): jnp.dot(matrix, row_panel, precision=lax.Precision.HIGHEST, preferred_ele...  60.4 us
    reduce_scatter x1, waiting for transfers between devices, shards(): lax.psum_scatter(partial_proj, 'row', scatter_dimension=0, tiled=True)  26.8 us
    dot_general x1, matrix products, shards(): lax.dot_general(lax.all_gather(basis_vectors, ('col', 'sub'), axis=1, til...  11 us
  transfers between devices with their start and end apart: 4, of which 3 were waited for; matrix products, arithmetic and copies ran while one was open for 14% of the time, Pallas kernels for 0%

commit v1 on v0

--- a/solution.py
+++ b/solution.py
@@ -4,8 +4,19 @@
 from jax.sharding import PartitionSpec as P
 
 
+def pass_along(x, mesh_axis, dim):
+    size = lax.axis_size(mesh_axis)
+    forward = [(i, (i + 1) % size) for i in range(size)]
+    parts = [x]
+    for far in range(1, size):
+        parts = [lax.ppermute(parts[0], mesh_axis, forward), *parts]
+    whole = jnp.concatenate(parts, axis=dim)
+    shift = (lax.axis_index(mesh_axis) + 1) * parts[-1].shape[dim]
+    return jnp.roll(whole, shift, axis=dim)
+
+
 def shards(matrix, basis_vectors, split_size):
-    strip = lax.all_gather(basis_vectors, "row", axis=0, tiled=True)
+    strip = pass_along(basis_vectors, "row", 0)
     row_panel = lax.all_to_all(strip, ("col", "sub"), split_axis=0, concat_axis=1, tiled=True)
     partial_image = jnp.dot(
         matrix, row_panel, precision=lax.Precision.HIGHEST, preferred_element_type=jnp.float32

time: 494 us -> 473 us (0.957)
  blocking collectives: 148 us -> 99.3 us
  local copies, waits for them, and re-layouts: 9.76 us -> 36.3 us
  waiting for transfers between devices: 250 us -> 240 us
  matrix products: 71.4 us -> 80 us
    all_gather x1 -> x0, waiting for transfers between devices: 153 us -> none  [shards(): strip = lax.all_gather(basis_vectors, 'row', axis=0, tiled=True)]
    ppermute x0 -> x3, waiting for transfers between devices: none -> 145 us  [pass_along(): parts = [lax.ppermute(parts[0], mesh_axis, forward), *parts]]
    all_to_all x1, blocking collectives: 145 us -> 96.9 us  [shards(): lax.all_to_all(strip, ('col', 'sub'), split_axis=0, concat_axis=1, tiled=...]
    unnamed x0 -> x13, local copies, waits for them, and re-layouts: none -> 21.2 us
    dot_general x1, matrix products: 60.4 us -> 68.8 us  [shards(): jnp.dot(matrix, row_panel, precision=lax.Precision.HIGHEST, preferred_ele...]
  transfers between devices with their start and end apart: 4 -> 6, of which waited for: 3 -> 5; matrix products, arithmetic and copies ran while one was open for 14% -> 22% of each run, Pallas kernels for 0% -> 0%
where the time goes in v1:
time: 473 us
  waiting for transfers between devices  240 us (51%)
  blocking collectives  99.3 us (21%)
  matrix products  80 us (17%)
  local copies, waits for them, and re-layouts  36.3 us (8%)
  between operations  13.8 us (3%)
    ppermute x3, waiting for transfers between devices, pass_along(): parts = [lax.ppermute(parts[0], mesh_axis, forward), *parts]  145 us
    all_to_all x1, blocking collectives, shards(): lax.all_to_all(strip, ('col', 'sub'), split_axis=0, concat_axis=1, tiled=...  96.9 us
    dot_general x1, matrix products, shards(): jnp.dot(matrix, row_panel, precision=lax.Precision.HIGHEST, preferred_ele...  68.8 us
    reduce_scatter x1, waiting for transfers between devices, shards(): lax.psum_scatter(partial_image, ('col', 'sub'), scatter_dimension=1, tile...  68.5 us
    reduce_scatter x1, waiting for transfers between devices, shards(): lax.psum_scatter(partial_proj, 'row', scatter_dimension=0, tiled=True)  26.8 us
    unnamed x13, local copies, waits for them, and re-layouts  21.2 us
    dot_general x1, matrix products, shards(): lax.dot_general(lax.all_gather(basis_vectors, ('col', 'sub'), axis=1, til...  11.1 us
  transfers between devices with their start and end apart: 6, of which 5 were waited for; matrix products, arithmetic and copies ran while one was open for 22% of the time, Pallas kernels for 0%

profile of v1, /device:TPU:0, one launch (start us, length us, event | category | flops | bytes accessed | tf_op | source)
XLA Modules:
  0.0 472.6 jit_solution(14732076714837908464)
XLA Ops:
  6.5 0.0 copy-start
  6.5 0.0 all-gather.2.cloned.1.call-start
  6.5 3.1 collective-permute-start
  9.6 47.9 %collective-permute-done = f32[2048,256]{1,0:T(8,128)S(1)} collective-permute-done((f32[2048,256]{1,0:T(8,128)}, f32[2048,256]{1,0:T(8,128)S(1)}, u32[]{:S(2)}, u32[]{:S(2)}) %collective-permute-start) | collective-permute-done | bytes 2097184 | tf_op jit(solution)/shard_map/ppermute | solution.py:12
  57.5 0.0 copy-start.1
  57.5 1.4 copy-done.1
  58.9 0.0 collective-permute-start.1
  58.9 48.7 %collective-permute-done.1 = f32[2048,256]{1,0:T(8,128)} collective-permute-done((f32[2048,256]{1,0:T(8,128)S(1)}, f32[2048,256]{1,0:T(8,128)}, u32[]{:S(2)}, u32[]{:S(2)}) %collective-permute-start.1) | collective-permute-done | bytes 2097184 | tf_op jit(solution)/shard_map/ppermute | solution.py:12
  107.6 0.0 collective-permute-start.2
  107.6 0.0 all-gather.2.cloned.1.call-update
  107.6 0.0 reduce-scatter.3.cloned.1.call-start
  107.7 0.0 copy-start.2
  107.7 47.9 %collective-permute-done.2 = f32[2048,256]{1,0:T(8,128)} collective-permute-done((f32[2048,256]{1,0:T(8,128)}, f32[2048,256]{1,0:T(8,128)}, u32[]{:S(2)}, u32[]{:S(2)}) %collective-permute-start.2) | collective-permute-done | bytes 2097184 | tf_op jit(solution)/shard_map/ppermute | solution.py:12
  155.6 3.1 constant_dynamic-update-slice_fusion.7
  158.7 3.0 constant_dynamic-update-slice_fusion.6
  161.7 3.0 constant_dynamic-update-slice_fusion.5
  164.8 3.1 constant_dynamic-update-slice_fusion.4
  167.9 3.1 constant_dynamic-update-slice_fusion.3
  171.0 3.0 constant_dynamic-update-slice_fusion.2
  174.0 0.0 copy-done.2
  174.0 1.5 constant_dynamic-update-slice_fusion.1
  175.5 0.0 copy-done
  175.5 1.4 constant_dynamic-update-slice_fusion
  176.9 3.9 constant_dynamic-slice_fusion
  180.8 96.9 %all_to_all.19 = f32[4,2048,256]{2,1,0:T(8,128)} all-to-all(f32[4,2048,256]{2,1,0:T(8,128)S(1)} %bitcast.16), channel_id=1, replica_groups=mesh['groups'=2,'row'=4,'col'=2,'sub'=2] {'col','sub'}, dimensions={0} | all-to-all | bytes 16777216 | tf_op jit(solution)/shard_map/all_to_all | solution.py:20
  277.7 8.8 %copy.6 = f32[2048,4,256]{0,2,1:T(8,128)} copy(f32[2048,4,256]{2,0,1:T(8,128)} %bitcast.17) | data formatting | bytes 16777216 | tf_op jit(solution)/shard_map/all_to_all | solution.py:20
  286.5 68.8 %convolution_bitcast_fusion = f32[2048,1024]{0,1:T(8,128)} fusion(f32[2048,1024]{0,1:T(8,128)} %bitcast.18, f32[2048,2048]{1,0:T(8,128)} %param.3), kind=kOutput, calls=%fused_computation | convolution fusion | flops 51539607552 | bytes 33554432 | tf_op jit(solution)/shard_map/dot_general | solution.py:21
  355.3 0.0 reduce-scatter.3.cloned.1.call-update
  355.3 0.0 reduce-scatter.5.cloned.1.call-start
  355.4 0.0 all-gather.2.cloned.1.call-done
  355.4 68.5 %reduce-scatter.3.cloned.1.call-done = f32[2048,256]{0,1:T(8,128)} async-done(((f32[2048,1024]{0,1:T(8,128)}), f32[2048,256]{0,1:T(8,128)}) %reduce-scatter.3.cloned.1.call-update) | async-done | bytes 2097168 | tf_op jit(solution)/shard_map/reduce_scatter | solution.py:24
  423.9 11.1 %convolution_bitcast_fusion.1 = f32[1024,256]{0,1:T(8,128)} fusion(f32[2048,256]{0,1:T(8,128)} %reduce-scatter.3.cloned.1.call-done, f32[2048,1024]{1,0:T(8,128)} %all-gather.2.cloned.1.call-done), kind=kOutput, calls=%fused_computation.1 | convolution fusion | flops 6442450944 | bytes 11534336 | tf_op jit(solution)/shard_map/dot_general | solution.py:25
  435.0 0.0 reduce-scatter.5.cloned.1.call-update
  435.7 26.8 %reduce-scatter.5.cloned.1.call-done = f32[256,256]{0,1:T(8,128)} async-done(((f32[1024,256]{0,1:T(8,128)}), f32[256,256]{0,1:T(8,128)}) %reduce-scatter.5.cloned.1.call-update) | async-done | bytes 262160 | tf_op jit(solution)/shard_map/reduce_scatter | solution.py:32
  462.5 2.4 all_gather.7
  464.9 0.2 select_bitcast_fusion
  465.1 1.0 copy.7
  (2 shorter events, 0.0 us)
Async XLA Ops:
  6.5 168.9 %copy-start = (f32[2048,256]{1,0:T(8,128)S(1)}, f32[2048,256]{1,0:T(8,128)}, u32[]{:S(2)}) copy-start(f32[2048,256]{1,0:T(8,128)} %param.4) | copy-start | bytes 6291460
  6.5 348.9 %all-gather.2.cloned.1.call-start = ((), (), s32[]{:S(2)}) async-start(), calls=%async_computation.4 | async-start | bytes 10485760 | tf_op jit(solution)/shard_map/all_gather | solution.py:26
  6.5 51.0 %collective-permute-start = (f32[2048,256]{1,0:T(8,128)}, f32[2048,256]{1,0:T(8,128)S(1)}, u32[]{:S(2)}, u32[]{:S(2)}) collective-permute-start(f32[2048,256]{1,0:T(8,128)} %param.4), channel_id=1, source_target_pairs={{0,4},{4,8},{8,12},{12,0},{1,5},{5,9},{9,13},{13,1},{2,6},{6,10},{... | collective-permute-start | bytes 6291464 | tf_op jit(solution)/shard_map/ppermute | solution.py:12
  57.5 1.4 copy-start.1
  58.9 48.7 %collective-permute-start.1 = (f32[2048,256]{1,0:T(8,128)S(1)}, f32[2048,256]{1,0:T(8,128)}, u32[]{:S(2)}, u32[]{:S(2)}) collective-permute-start(f32[2048,256]{1,0:T(8,128)S(1)} %collective-permute-done), channel_id=1, source_target_pairs={{0,4},{4,8},{8,12},{12,0},{1,5},{5,9},{9,13},{13,1},{2,6},{6,10},{... | collective-permute-start | bytes 6291464 | tf_op jit(solution)/shard_map/ppermute | solution.py:12
  107.6 48.1 %collective-permute-start.2 = (f32[2048,256]{1,0:T(8,128)}, f32[2048,256]{1,0:T(8,128)}, u32[]{:S(2)}, u32[]{:S(2)}) collective-permute-start(f32[2048,256]{1,0:T(8,128)} %collective-permute-done.1), channel_id=1, source_target_pairs={{0,4},{4,8},{8,12},{12,0},{1,5},{5,9},{9,13},{13,1},{2,6},{6,10},{... | collective-permute-start | bytes 6291464 | tf_op jit(solution)/shard_map/ppermute | solution.py:12
  107.6 316.3 %reduce-scatter.3.cloned.1.call-start = ((), (), s32[]{:S(2)}) async-start(), calls=%async_computation.3 | async-start | bytes 10485760 | tf_op jit(solution)/shard_map/reduce_scatter | solution.py:24
  107.7 66.3 %copy-start.2 = (f32[2048,256]{1,0:T(8,128)S(1)}, f32[2048,256]{1,0:T(8,128)}, u32[]{:S(2)}) copy-start(f32[2048,256]{1,0:T(8,128)} %copy-done.1) | copy-start | bytes 6291460
  355.3 107.1 %reduce-scatter.5.cloned.1.call-start = ((), (), s32[]{:S(2)}) async-start(), calls=%async_computation.5 | async-start | bytes 1310720 | tf_op jit(solution)/shard_map/reduce_scatter | solution.py:32
Sparse Core Ops, SparseCore 0:
  107.7 59.5 all-gather.1
  355.5 68.3 reduce-scatter.2
  435.1 27.2 reduce-scatter.4
